TPU v7x, 32 devices: a whole 2x2x4 slice. The times are simulated.
32 devices in a mesh: dp: 2 (over x), expert: 16 (over z, y, core).
Axes of the slice: x: 2, y: 2, z: 4, core: 2. Of those that a mesh axis runs over, the one named last changes fastest.
Arguments:
- tokens: bfloat16 [3072, 2048], P(('dp', 'expert')), may hold values from -6 to 6
- routes: int32 [3072, 8], P(('dp', 'expert')), may hold values from 0 to 15, all different within a row; in each aligned block of 96 rows (0 to 95, 96 to 191, ...) at most 64 rows name the same one
- weights: bfloat16 [16, 2, 768, 2048], P('expert', None, 'dp'), may hold values from -0.125 to 0.125
- keep_mask: int32 [16, 2, 768, 128], P('expert', None, 'dp'), may hold values from 0 to 1, as said below
- inv_factor: float32 [16, 128, 2048], P('expert'), as said below
Outputs:
- hidden: bfloat16 [3072, 8, 768], P(('dp', 'expert'))
Inputs may be any that keep to these rules, and one draw needn't show every extreme that they name: `routes`: each token names 8 different experts; the 96 rows of one device name any one expert at most 64 times. `keep_mask`: each row of 128 entries holds exactly 64 ones. `inv_factor`: each expert's factor is upper triangular: entry (i, j) is zero for j < i, and the diagonal entry (i, i) lies in [0.6, 1.6].
All inputs are finite; a program needn't handle non-finite values.
Results may differ from a plain program's by a relative error of at most 0.0058.
Values may be sent and summed in bfloat16 or wider, within the bound.
A program may use at most 64 MiB of HBM per device.

v0:
```python
import jax
import jax.numpy as jnp
from jax import lax
from jax.sharding import PartitionSpec as P


def prune_rows(weights, keep_mask, inv_factor):
    block_width = keep_mask.shape[-1]
    initial = weights.astype(jnp.float32)
    leading = initial[..., :block_width]
    dropped = (1 - keep_mask).astype(jnp.float32)
    factor_block = inv_factor[:, :, :block_width]

    def column(column_id, state):
        leading, errors = state
        current = lax.dynamic_index_in_dim(leading, column_id, 3, keepdims=False)
        factor_row = lax.dynamic_index_in_dim(factor_block, column_id, 1, keepdims=False)
        diagonal = lax.dynamic_index_in_dim(factor_row, column_id, 1, keepdims=False)
        error_col = (
            lax.dynamic_index_in_dim(dropped, column_id, 3, keepdims=False)
            * current
            / diagonal[:, None, None]
        )
        leading = leading - error_col[..., None] * factor_row[:, None, None, :]
        errors = lax.dynamic_update_index_in_dim(errors, error_col, column_id, 3)
        return (leading, errors)

    leading, errors = lax.fori_loop(0, block_width, column, (leading, jnp.zeros_like(leading)))
    trailing = initial[..., block_width:] - jnp.einsum(
        "epri,eij->eprj", errors, inv_factor[:, :, block_width:], precision=lax.Precision.HIGHEST
    )
    return jnp.concatenate([leading, trailing], axis=-1).astype(jnp.bfloat16)


def local(tokens, routes, weights, keep_mask, inv_factor):
    pruned = prune_rows(weights, keep_mask, inv_factor)
    gate_all = lax.all_gather(pruned[0, 0], "dp", axis=0, tiled=True)
    up_all = lax.all_gather(pruned[0, 1], "dp", axis=0, tiled=True)
    owners = lax.axis_size("expert")
    token_rows = tokens.shape[0]
    top_count = routes.shape[1]
    model_width = tokens.shape[1]
    capacity = token_rows * top_count * 4 // (3 * owners)
    slot_expert = routes.reshape(-1)
    one_hot = (slot_expert[:, None] == jnp.arange(owners, dtype=jnp.int32)[None, :]).astype(
        jnp.int32
    )
    slot_rank = jnp.sum(jnp.cumsum(one_hot, axis=0) * one_hot, axis=1) - 1
    target = slot_expert * capacity + slot_rank
    source = jnp.arange(slot_expert.shape[0], dtype=jnp.int32) // top_count
    outbox = (
        jnp.zeros((owners * capacity, model_width), jnp.bfloat16).at[target].set(tokens[source])
    )
    outbox = outbox.reshape(owners, capacity, model_width)
    arrived = lax.all_to_all(outbox, "expert", split_axis=0, concat_axis=0, tiled=True)
    arrived_rows = arrived.reshape(-1, model_width)
    gate_out = lax.dot_general(
        arrived_rows, gate_all, (((1,), (1,)), ((), ())), preferred_element_type=jnp.float32
    )
    up_out = lax.dot_general(
        arrived_rows, up_all, (((1,), (1,)), ((), ())), preferred_element_type=jnp.float32
    )
    hidden_rows = (jax.nn.silu(gate_out) * up_out).astype(jnp.bfloat16)
    hidden_rows = hidden_rows.reshape(arrived.shape[0], arrived.shape[1], -1)
    results = lax.all_to_all(hidden_rows, "expert", split_axis=0, concat_axis=0, tiled=True)
    hidden = results.reshape(owners * capacity, -1)[target]
    return hidden.reshape(token_rows, top_count, -1)


def solution(mesh):
    return jax.shard_map(
        local,
        mesh=mesh,
        in_specs=(
            P(("dp", "expert"), None),
            P(("dp", "expert"), None),
            P("expert", None, "dp", None),
            P("expert", None, "dp", None),
            P("expert", None, None),
        ),
        out_specs=P(("dp", "expert"), None, None),
        check_vma=False,
    )
```

profile of v0, /device:TPU:15, one launch (start us, length us, event | category | flops | bytes accessed | tf_op | source)
XLA Modules:
  0.0 462.8 jit_solution(8437332724690779670)
XLA Ops:
  8.5 1.7 reduce-window.6
  10.6 22.9 %scatter_custom_fusion = bf16[1024,2048]{1,0:T(8,128)(2,1)} fusion(s32[768]{0:T(1024)S(1)} %fusion.18, bf16[96,2048]{1,0:T(8,128)(2,1)S(1)} %copy-done, s32[1024]{0:T(1024)S(1)} %pad_clamp_fusion.1, bf16[]{:T(256)} %constant.139.clone.1), kind=kCustom, calls=%fused_computation.17 | custom fusion | bytes 4194306 | tf_op jit(solution)/shard_map/scatter | solution.py:52
  33.5 6.7 %all-to-all-start = ((bf16[16,64,2048]{2,1,0:T(8,128)(2,1)}), bf16[16,64,2048]{2,1,0:T(8,128)(2,1)}, u32[]{:S(2)}, u32[]{:S(2)}) async-start(bf16[16,64,2048]{2,1,0:T(8,128)(2,1)} %bitcast.50), calls=%async_computation | async-start | bytes 8388608 | tf_op jit(solution)/shard_map/all_to_all | solution.py:55
  40.6 1.0 slice.37
  41.8 253.1 %while.18 = (s32[]{:T(128)}, f32[1,2,384,128]{2,1,3,0:T(2,128)S(1)}, f32[1,2,384,128]{2,1,3,0:T(2,128)S(1)}, f32[1,2,384,128]{2,1,3,0:T(2,128)S(1)}, f32[1,128,1...) while((s32[]{:T(128)}, f32[1,2,384,128]{2,1,3,0:T(2,128)S(1)}, f32[1,2,384,128]{2,1,3,0:T(2,128)S(1)}, ...), condition=%wide.region_5.6_spmd, body=%wide.region_4.5_spmd.sunk | while | flops 198147 | bytes 803461 | solution.py:28
  44.9 0.8 multiply_subtract_fusion.2
  50.9 0.8 multiply_subtract_fusion.2
  54.8 0.8 multiply_subtract_fusion.2
  64.7 0.8 multiply_subtract_fusion.2
  68.7 0.8 multiply_subtract_fusion.2
  78.5 0.8 multiply_subtract_fusion.2
  82.5 0.8 multiply_subtract_fusion.2
  88.4 0.8 multiply_subtract_fusion.2
  92.4 0.8 multiply_subtract_fusion.2
  102.3 0.8 multiply_subtract_fusion.2
  106.2 0.8 multiply_subtract_fusion.2
  116.1 0.8 multiply_subtract_fusion.2
  120.1 0.8 multiply_subtract_fusion.2
  126.0 0.8 multiply_subtract_fusion.2
  130.0 0.8 multiply_subtract_fusion.2
  139.8 0.8 multiply_subtract_fusion.2
  143.8 0.8 multiply_subtract_fusion.2
  294.9 5.5 %convert_element_type.24 = f32[1,2,384,2048]{3,2,1,0:T(8,128)} convert(bf16[1,2,384,2048]{3,2,1,0:T(8,128)(2,1)} %param.9) | non-fusion elementwise | flops 1572864 | bytes 9437184 | tf_op jit(solution)/shard_map/convert_element_type | solution.py:9
  300.7 6.9 %fusion.1 = bf16[1,2,384,1920]{3,2,1,0:T(8,128)(2,1)S(1)} fusion(f32[1,2,384,2048]{3,2,1,0:T(8,128)} %convert_element_type.24, f32[1,128,2048]{2,1,0:T(8,128)S(1)} %copy-done.1, f32[2,384,128]{1,0,2:T(2,128)S(1)} %bitcast.51), kind=kOutput, calls=%fused_computation.10 | convolution fusion | flops 2267873280 | bytes 10223616 | tf_op jit(solution)/shard_map/epri,eij->eprj/dot_general | solution.py:29
  307.6 2.2 fusion.11
  310.5 43.8 %all-gather.7.cloned.1.call-done = bf16[1,1,768,2048]{3,2,1,0:T(8,128)(2,1)} async-done(((bf16[1,1,384,2048]{3,2,1,0:T(8,128)(2,1)}), bf16[1,1,768,2048]{3,2,1,0:T(8,128)(2,1)}) %all-gather.7.cloned.1.call-update) | async-done | bytes 3145744 | tf_op jit(solution)/shard_map/all_gather | solution.py:38
  354.3 8.3 %fusion.2 = f32[1024,768]{1,0:T(8,128)} fusion(bf16[1024,2048]{1,0:T(8,128)(2,1)} %bitcast.5, bf16[1,1,768,2048]{3,2,1,0:T(8,128)(2,1)} %all-gather.7.cloned.1.call-done), kind=kOutput, calls=%fused_computation.13 | convolution fusion | flops 3221225472 | bytes 10485760 | tf_op jit(solution)/shard_map/dot_general | solution.py:60
  362.6 38.2 %all-gather.5.cloned.1.call-done = bf16[1,1,768,2048]{3,2,1,0:T(8,128)(2,1)} async-done(((bf16[1,1,384,2048]{3,2,1,0:T(8,128)(2,1)}), bf16[1,1,768,2048]{3,2,1,0:T(8,128)(2,1)}) %all-gather.5.cloned.1.call-update) | async-done | bytes 3145744 | tf_op jit(solution)/shard_map/all_gather | solution.py:37
  400.8 9.0 %multiply_convert_fusion = bf16[1024,768]{1,0:T(8,128)(2,1)} fusion(f32[1024,768]{1,0:T(8,128)} %fusion.2, bf16[1024,2048]{1,0:T(8,128)(2,1)} %bitcast.5, bf16[1,1,768,2048]{3,2,1,0:T(8,128)(2,1)} %all-gather.5.cloned.1.call-done), kind=kOutput, calls=%fused_computation.19 | convolution fusion | flops 3225944064 | bytes 12058624 | tf_op jit(solution)/shard_map/dot_general | solution.py:57
  409.8 6.5 %all-to-all-start.1 = ((bf16[16,64,768]{2,1,0:T(8,128)(2,1)}), bf16[16,64,768]{2,1,0:T(8,128)(2,1)S(1)}, u32[]{:S(2)}, u32[]{:S(2)}) async-start(bf16[16,64,768]{2,1,0:T(8,128)(2,1)} %bitcast.12), calls=%async_computation.1 | async-start | bytes 3145728 | tf_op jit(solution)/shard_map/all_to_all | solution.py:65
  416.3 36.2 %all-to-all-done.1 = bf16[16,64,768]{2,1,0:T(8,128)(2,1)S(1)} async-done(((bf16[16,64,768]{2,1,0:T(8,128)(2,1)}), bf16[16,64,768]{2,1,0:T(8,128)(2,1)S(1)}, u32[]{:S(2)}, u32[]{:S(2)}) %all-to-all-start.1) | async-done | bytes 1572896 | tf_op jit(solution)/shard_map/all_to_all | solution.py:65
  452.5 3.4 gather_fusion
  (528 shorter events, 241.1 us)
Async XLA Ops:
  6.5 4.1 copy-start
  33.5 6.7 %copy-start.2 = (s32[1,2,384,128]{3,2,1,0:T(8,128)S(1)}, s32[1,2,384,128]{3,2,1,0:T(8,128)}, u32[]{:S(2)}) copy-start(s32[1,2,384,128]{3,2,1,0:T(8,128)} %param.10) | copy-start | bytes 1179652
  33.5 320.8 %all-to-all-start = ((bf16[16,64,2048]{2,1,0:T(8,128)(2,1)}), bf16[16,64,2048]{2,1,0:T(8,128)(2,1)}, u32[]{:S(2)}, u32[]{:S(2)}) async-start(bf16[16,64,2048]{2,1,0:T(8,128)(2,1)} %bitcast.50), calls=%async_computation | async-start | bytes 8388608 | tf_op jit(solution)/shard_map/all_to_all | solution.py:55
  40.1 1.6 slice-start
  40.1 314.2 %all-gather.7.cloned.1.call-start = ((), (), s32[]{:S(2)}) async-start(), calls=%async_computation.3 | async-start | bytes 4718592 | tf_op jit(solution)/shard_map/all_gather | solution.py:38
  294.9 5.7 %copy-start.1 = (f32[1,128,2048]{2,1,0:T(8,128)S(1)}, f32[1,128,2048]{2,1,0:T(8,128)}, u32[]{:S(2)}) copy-start(f32[1,128,2048]{2,1,0:T(8,128)} %param.11) | copy-start | bytes 3145732
  309.8 91.1 %all-gather.5.cloned.1.call-start = ((), (), s32[]{:S(2)}) async-start(), calls=%async_computation.2 | async-start | bytes 4718592 | tf_op jit(solution)/shard_map/all_gather | solution.py:37
  409.8 42.7 %all-to-all-start.1 = ((bf16[16,64,768]{2,1,0:T(8,128)(2,1)}), bf16[16,64,768]{2,1,0:T(8,128)(2,1)S(1)}, u32[]{:S(2)}, u32[]{:S(2)}) async-start(bf16[16,64,768]{2,1,0:T(8,128)(2,1)} %bitcast.12), calls=%async_computation.1 | async-start | bytes 3145728 | tf_op jit(solution)/shard_map/all_to_all | solution.py:65
Sparse Core Ops, SparseCore 0:
  309.9 44.4 all-gather.6
  355.9 44.8 all-gather.4
where the time goes:
time: 465 us; the launch traced here: 463 us
  other arithmetic  189 us (41%)
  waiting for transfers between devices  119 us (26%)
  local copies, waits for them, and re-layouts  102 us (22%)
  matrix products  24.2 us (5%)
  between operations  13.6 us (3%)
  starting transfers between devices  13.2 us (3%)
    sub x128, other arithmetic, column(): leading = leading - error_col[..., None] * factor_row[:, None, None, :]  104 us
    dynamic_update_slice x128, other arithmetic, column(): errors = lax.dynamic_update_index_in_dim(errors, error_col, column_id, 3)  74.7 us
    dynamic_slice x128, local copies, waits for them, and re-layouts, column(): lax.dynamic_index_in_dim(factor_row, column_id, 1, keepdims=False)  71.7 us
    all_gather x1, waiting for transfers between devices, local(): up_all = lax.all_gather(pruned[0, 1], 'dp', axis=0, tiled=True)  43.8 us
    all_gather x1, waiting for transfers between devices, local(): gate_all = lax.all_gather(pruned[0, 0], 'dp', axis=0, tiled=True)  38.2 us
    all_to_all x1, waiting for transfers between devices, local(): lax.all_to_all(hidden_rows, 'expert', split_axis=0, concat_axis=0, tiled=...  36.2 us
    scatter x1, local copies, waits for them, and re-layouts, local(): jnp.zeros((owners * capacity, model_width), jnp.bfloat16).at[target]  22.9 us
  transfers between devices with their start and end apart: 4, of which 3 were waited for; matrix products, arithmetic and copies ran while one was open for 60% of the time, Pallas kernels for 0%

commit v1 on v0

v1 whole, which is shorter than its diff:
```python
import functools

import jax
import jax.numpy as jnp
from jax import lax
from jax.experimental import pallas as pl
from jax.experimental.pallas import tpu as pltpu
from jax.sharding import PartitionSpec as P

SUB = 8
LANES = 128
GATHER_LIMIT = 24 << 20
VMEM = pltpu.VMEM


def prune_kernel(w_ref, mask_ref, f_ref, out_ref, u_ref, e_ref, m_ref, ft_ref, lhs_ref, rhs_ref):
    rows, width = w_ref.shape
    block = mask_ref.shape[1]
    blocks = block // SUB
    u_ref[...] = w_ref[:, :block].astype(jnp.float32).T
    factor = f_ref[:, :block]
    eye = lax.broadcasted_iota(jnp.int32, (block, block), 0) == lax.broadcasted_iota(
        jnp.int32, (block, block), 1
    )
    diagonal = jnp.sum(jnp.where(eye, factor, 0.0), axis=1, keepdims=True)
    m_ref[...] = (1 - mask_ref[...]).astype(jnp.float32).T * (1.0 / diagonal)
    factor_t = factor.T
    for b in range(blocks):
        ft_ref[b, :, :SUB] = factor_t[:, b * SUB : (b + 1) * SUB]

    def outer(b, carry):
        start = pl.multiple_of(b * SUB, SUB)
        u = u_ref[pl.ds(start, SUB), :]
        m = m_ref[pl.ds(start, SUB), :]
        ft = ft_ref[b, pl.ds(start, SUB), :SUB]
        errors = []
        for s in range(SUB):
            error = jnp.broadcast_to(m[s : s + 1] * u[s : s + 1], (SUB, rows))
            u = u - ft[:, s : s + 1] * error
            errors.append(error)
        u_ref[pl.ds(start, SUB), :] = u
        sub_ids = lax.broadcasted_iota(jnp.int32, (SUB, rows), 0)
        stacked = errors[0]
        for s in range(1, SUB):
            stacked = jnp.where(sub_ids == s, errors[s], stacked)
        e_ref[pl.ds(start, SUB), :] = stacked

        def inner(c, carry):
            place = pl.multiple_of(c * SUB, SUB)
            later = u_ref[pl.ds(place, SUB), :]
            column = ft_ref[b, pl.ds(place, SUB), :SUB]
            for s in range(SUB):
                later = later - column[:, s : s + 1] * errors[s]
            u_ref[pl.ds(place, SUB), :] = later
            return carry

        return lax.fori_loop(b + 1, blocks, inner, carry)

    lax.fori_loop(0, blocks, outer, 0)
    errors = e_ref[...].T
    high = errors.astype(jnp.bfloat16)
    low = (errors - high.astype(jnp.float32)).astype(jnp.bfloat16)
    lhs_ref[:, :block] = high
    lhs_ref[:, block : 2 * block] = low
    lhs_ref[:, 2 * block :] = high
    f_high = f_ref[...].astype(jnp.bfloat16)
    f_low = (f_ref[...] - f_high.astype(jnp.float32)).astype(jnp.bfloat16)
    rhs_ref[:block] = f_high
    rhs_ref[block : 2 * block] = f_high
    rhs_ref[2 * block :] = f_low
    out_ref[:, :block] = u_ref[...].T.astype(jnp.bfloat16)
    tile = next(t for t in (3 * LANES, 2 * LANES, LANES) if (width - block) % t == 0)

    def trail(c, carry):
        cols = pl.ds(pl.multiple_of(block + c * tile, LANES), tile)
        change = jnp.dot(lhs_ref[...], rhs_ref[:, cols], preferred_element_type=jnp.float32)
        out_ref[:, cols] = (w_ref[:, cols].astype(jnp.float32) - change).astype(jnp.bfloat16)
        return carry

    lax.fori_loop(0, (width - block) // tile, trail, 0)


def prune(weights, keep_mask, inv_factor):
    rows, width = weights.shape
    block = keep_mask.shape[1]
    return pl.pallas_call(
        prune_kernel,
        out_shape=jax.ShapeDtypeStruct((rows, width), jnp.bfloat16),
        in_specs=[pl.BlockSpec(memory_space=VMEM)] * 3,
        out_specs=pl.BlockSpec(memory_space=VMEM),
        scratch_shapes=[
            VMEM((block, rows), jnp.float32),
            VMEM((block, rows), jnp.float32),
            VMEM((block, rows), jnp.float32),
            VMEM((block // SUB, block, LANES), jnp.float32),
            VMEM((rows, 3 * block), jnp.bfloat16),
            VMEM((3 * block, width), jnp.bfloat16),
        ],
        cost_estimate=pl.CostEstimate(
            flops=6 * rows * block * width, bytes_accessed=4 * rows * width, transcendentals=0
        ),
        name="prune",
    )(weights, keep_mask, inv_factor)


def apply_kernel(capacity, token_rows, x_ref, w_ref, out_ref):
    width = w_ref.shape[1]
    half = w_ref.shape[0] // 2
    expert = lax.axis_index("expert")
    x = x_ref[:, :width]
    both = lax.dot_general(
        x, w_ref[...], (((1,), (1,)), ((), ())), preferred_element_type=jnp.float32
    )
    gate, up = both[:, :half], both[:, half:]
    hidden = (gate / (1.0 + jnp.exp(-gate)) * up).astype(jnp.bfloat16)
    ranks = x_ref[:, width:].astype(jnp.float32)
    lane = lax.broadcasted_iota(jnp.int32, ranks.shape, 1)
    rank = jnp.sum(jnp.where(lane == expert, ranks, 0.0), axis=1, keepdims=True).astype(jnp.int32)
    slots = lax.broadcasted_iota(jnp.int32, (x.shape[0], capacity), 1)
    pick = jnp.where(rank == slots, 1.0, 0.0).astype(jnp.bfloat16)
    for j in range(x.shape[0] // token_rows):
        part = slice(j * token_rows, (j + 1) * token_rows)
        out_ref[j] = lax.dot_general(
            pick[part], hidden[part], (((0,), (0,)), ((), ())), preferred_element_type=jnp.float32
        ).astype(jnp.bfloat16)


def combine_kernel(target_ref, got_ref, out_ref):
    halves, slots, half = got_ref.shape
    place = lax.broadcasted_iota(jnp.int32, (target_ref.shape[0], slots), 1)
    pick = jnp.where(target_ref[...] == place, 1.0, 0.0).astype(jnp.bfloat16)
    for h in range(halves):
        out_ref[:, h * half : (h + 1) * half] = jnp.dot(
            pick, got_ref[h], preferred_element_type=jnp.float32
        ).astype(jnp.bfloat16)


def ranks_of(routes, owners):
    token_rows = routes.shape[0]
    ids = jnp.arange(owners, dtype=jnp.int32)
    hot = jnp.any(routes[:, :, None] == ids[None, None, :], axis=1)
    before = jnp.tril(jnp.ones((token_rows, token_rows), jnp.bfloat16), -1)
    rank = jnp.dot(before, hot.astype(jnp.bfloat16), preferred_element_type=jnp.float32)
    return jnp.where(hot, rank, -1.0)


def dense(tokens, routes, pruned, capacity):
    owners, groups = lax.axis_size("expert"), lax.axis_size("dp")
    token_rows, width = tokens.shape
    top = routes.shape[1]
    devices = owners * groups
    half = pruned.shape[0] // 2
    rank = ranks_of(routes, owners)
    extra = -owners % LANES
    tagged = jnp.concatenate(
        [tokens, jnp.pad(rank, ((0, 0), (0, extra))).astype(jnp.bfloat16)], axis=1
    )
    gathered = lax.all_gather(tagged, ("dp", "expert"), axis=0, tiled=True)
    many = next(m for m in (4, 2, 1) if devices % m == 0)
    packed = pl.pallas_call(
        functools.partial(apply_kernel, capacity, token_rows),
        grid=(devices // many,),
        out_shape=jax.ShapeDtypeStruct((devices, capacity, half), jnp.bfloat16),
        in_specs=[
            pl.BlockSpec((many * token_rows, tagged.shape[1]), lambda i: (i, 0)),
            pl.BlockSpec((2 * half, width), lambda i: (0, 0)),
        ],
        out_specs=pl.BlockSpec((many, capacity, half), lambda i: (i, 0, 0)),
        name="apply",
    )(gathered, pruned)
    got = lax.all_to_all(packed, ("dp", "expert"), split_axis=0, concat_axis=0, tiled=True)
    ids = jnp.arange(owners, dtype=jnp.int32)
    own_rank = jnp.sum(
        jnp.where(routes[:, :, None] == ids[None, None, :], rank[:, None, :], 0.0), axis=2
    ).astype(jnp.int32)
    target = (routes * capacity + own_rank).reshape(-1, 1)
    out = pl.pallas_call(
        combine_kernel,
        out_shape=jax.ShapeDtypeStruct((token_rows * top, groups * half), jnp.bfloat16),
        name="combine",
    )(target, got.reshape(groups, owners * capacity, half))
    return out.reshape(token_rows, top, groups * half)


def routed(tokens, routes, pruned, capacity):
    half = pruned.shape[0] // 2
    gate_all = lax.all_gather(pruned[:half], "dp", axis=0, tiled=True)
    up_all = lax.all_gather(pruned[half:], "dp", axis=0, tiled=True)
    owners = lax.axis_size("expert")
    token_rows, model_width = tokens.shape
    top_count = routes.shape[1]
    slot_expert = routes.reshape(-1)
    one_hot = (slot_expert[:, None] == jnp.arange(owners, dtype=jnp.int32)[None, :]).astype(
        jnp.int32
    )
    slot_rank = jnp.sum(jnp.cumsum(one_hot, axis=0) * one_hot, axis=1) - 1
    target = slot_expert * capacity + slot_rank
    source = jnp.arange(slot_expert.shape[0], dtype=jnp.int32) // top_count
    outbox = (
        jnp.zeros((owners * capacity, model_width), jnp.bfloat16).at[target].set(tokens[source])
    )
    outbox = outbox.reshape(owners, capacity, model_width)
    arrived = lax.all_to_all(outbox, "expert", split_axis=0, concat_axis=0, tiled=True)
    arrived_rows = arrived.reshape(-1, model_width)
    gate_out = lax.dot_general(
        arrived_rows, gate_all, (((1,), (1,)), ((), ())), preferred_element_type=jnp.float32
    )
    up_out = lax.dot_general(
        arrived_rows, up_all, (((1,), (1,)), ((), ())), preferred_element_type=jnp.float32
    )
    hidden_rows = (jax.nn.silu(gate_out) * up_out).astype(jnp.bfloat16)
    hidden_rows = hidden_rows.reshape(arrived.shape[0], arrived.shape[1], -1)
    results = lax.all_to_all(hidden_rows, "expert", split_axis=0, concat_axis=0, tiled=True)
    hidden = results.reshape(owners * capacity, -1)[target]
    return hidden.reshape(token_rows, top_count, -1)


def local(tokens, routes, weights, keep_mask, inv_factor):
    owners, groups = lax.axis_size("expert"), lax.axis_size("dp")
    token_rows, width = tokens.shape
    capacity = token_rows * routes.shape[1] * 4 // (3 * owners)
    pruned = prune(
        weights.reshape(-1, width),
        keep_mask.reshape(-1, keep_mask.shape[-1]),
        inv_factor.reshape(-1, width),
    )
    if 2 * owners * groups * tokens.size <= GATHER_LIMIT:
        return dense(tokens, routes, pruned, capacity)
    return routed(tokens, routes, pruned, capacity)


def solution(mesh):
    return jax.shard_map(
        local,
        mesh=mesh,
        in_specs=(
            P(("dp", "expert"), None),
            P(("dp", "expert"), None),
            P("expert", None, "dp", None),
            P("expert", None, "dp", None),
            P("expert", None, None),
        ),
        out_specs=P(("dp", "expert"), None, None),
        check_vma=False,
    )
```

time: 465 us -> 183 us (0.39)
  the two profiles are of different devices: /device:TPU:15 before, /device:TPU:0 now
where the time goes in v1:
time: 183 us
  waiting for transfers between devices  121 us (66%)
  Pallas kernels  40.4 us (22%)
  between operations  13.4 us (7%)
  starting transfers between devices  3.12 us (2%)
  other arithmetic  2.53 us (1%)
  local copies, waits for them, and re-layouts  2.35 us (1%)
    all_gather x1, waiting for transfers between devices, dense(): gathered = lax.all_gather(tagged, ('dp', 'expert'), axis=0, tiled=True)  83.2 us
    all_to_all x1, waiting for transfers between devices, dense(): lax.all_to_all(packed, ('dp', 'expert'), split_axis=0, concat_axis=0, til...  37.4 us
    pallas_call x1, Pallas kernels, prune(): pl.pallas_call(prune_kernel, out_shape=jax.ShapeDtypeStruct((rows, width)...  19.4 us
    pallas_call x1, Pallas kernels, dense(): pl.pallas_call(functools.partial(apply_kernel, capacity, token_rows), gri...  16.6 us
    pallas_call x1, Pallas kernels, dense(): pl.pallas_call(combine_kernel, out_shape=jax.ShapeDtypeStruct((token_rows...  4.38 us
  transfers between devices with their start and end apart: 2, of which 2 were waited for; matrix products, arithmetic and copies ran while one was open for 1% of the time, Pallas kernels for 11%

profile of v1, /device:TPU:0, one launch (start us, length us, event | category | flops | bytes accessed | tf_op | source)
XLA Modules:
  0.0 182.6 jit_solution(6120914709988393815)
XLA Ops:
  6.5 0.0 all-gather.2.cloned.1.call-start
  6.5 0.7 fusion.2
  7.2 0.1 copy.13
  7.3 0.2 fusion.10
  7.5 1.8 fusion.1
  9.3 0.0 all-gather.2.cloned.1.call-update
  9.4 19.4 %prune.1.w_ref = bf16[768,2048]{1,0:T(8,128)(2,1)} custom-call(bf16[768,2048]{1,0:T(8,128)(2,1)} %bitcast.7, s32[768,128]{1,0:T(8,128)} %bitcast.9, f32[128,2048]{1,0:T(8,128)} %bitcast.8), custom_call_target="tpu_custom_call" | custom-call | flops 1207959552 | bytes 6291456 | tf_op jit(solution)/shard_map/prune/pallas_call | solution.py:86
  28.7 83.2 %all-gather.2.cloned.1.call-done.x_ref = bf16[3072,2176]{1,0:T(8,128)(2,1)} async-done(((bf16[96,2176]{1,0:T(8,128)(2,1)}), bf16[3072,2176]{1,0:T(8,128)(2,1)}) %all-gather.2.cloned.1.call-update) | async-done | bytes 13369360 | tf_op jit(solution)/shard_map/all_gather | solution.py:158
  111.9 16.6 %apply.1 = bf16[32,64,384]{2,1,0:T(8,128)(2,1)} custom-call(bf16[3072,2176]{1,0:T(8,128)(2,1)} %all-gather.2.cloned.1.call-done.x_ref, bf16[768,2048]{1,0:T(8,128)(2,1)} %prune.1.w_ref), custom_call_target="tpu_custom_call" | custom-call | tf_op jit(solution)/shard_map/apply/pallas_call | solution.py:160
  128.5 0.0 copy-start.1
  128.6 3.1 %all-to-all-start = ((bf16[32,64,384]{2,1,0:T(8,128)(2,1)}), bf16[32,64,384]{2,1,0:T(8,128)(2,1)S(1)}, u32[]{:S(2)}, u32[]{:S(2)}) async-start(bf16[32,64,384]{2,1,0:T(8,128)(2,1)} %apply.1), calls=%async_computation | async-start | bytes 3145728 | tf_op jit(solution)/shard_map/all_to_all | solution.py:171
  131.7 0.1 copy.15
  131.7 0.0 copy-done.1
  131.8 0.1 copy.16
  131.9 0.9 reshape.26.target_ref
  132.8 37.4 %all-to-all-done = bf16[32,64,384]{2,1,0:T(8,128)(2,1)S(1)} async-done(((bf16[32,64,384]{2,1,0:T(8,128)(2,1)}), bf16[32,64,384]{2,1,0:T(8,128)(2,1)S(1)}, u32[]{:S(2)}, u32[]{:S(2)}) %all-to-all-start) | async-done | bytes 1572896 | tf_op jit(solution)/shard_map/all_to_all | solution.py:171
  170.2 0.0 copy-start
  170.2 1.2 copy-done
  171.4 4.4 %combine.1 = bf16[768,768]{1,0:T(8,128)(2,1)} custom-call(s32[768,1]{1,0:T(8,128)} %reshape.26.target_ref, bf16[2,1024,384]{2,1,0:T(8,128)(2,1)} %bitcast.6), custom_call_target="tpu_custom_call" | custom-call | tf_op jit(solution)/shard_map/combine/pallas_call | solution.py:177
  (3 shorter events, 0.0 us)
Async XLA Ops:
  6.5 105.4 %all-gather.2.cloned.1.call-start = ((), (), s32[]{:S(2)}) async-start(), calls=%async_computation.1 | async-start | bytes 13787136 | tf_op jit(solution)/shard_map/all_gather | solution.py:158
  128.5 3.2 %copy-start.1 = (s32[96,8]{0,1:T(8,128)S(1)}, s32[96,8]{0,1:T(8,128)}, u32[]{:S(2)}) copy-start(s32[96,8]{0,1:T(8,128)} %param.6) | copy-start | bytes 9220
  128.6 41.7 %all-to-all-start = ((bf16[32,64,384]{2,1,0:T(8,128)(2,1)}), bf16[32,64,384]{2,1,0:T(8,128)(2,1)S(1)}, u32[]{:S(2)}, u32[]{:S(2)}) async-start(bf16[32,64,384]{2,1,0:T(8,128)(2,1)} %apply.1), calls=%async_computation | async-start | bytes 3145728 | tf_op jit(solution)/shard_map/all_to_all | solution.py:171
  170.2 1.2 copy-start
Sparse Core Ops, SparseCore 0:
  10.2 101.6 all-gather.1

commit v2 on v1

--- a/solution.py
+++ b/solution.py
@@ -13,10 +13,8 @@
 VMEM = pltpu.VMEM
 
 
-def prune_kernel(w_ref, mask_ref, f_ref, out_ref, u_ref, e_ref, m_ref, ft_ref, lhs_ref, rhs_ref):
-    rows, width = w_ref.shape
+def prune_setup(w_ref, mask_ref, f_ref, u_ref, m_ref, ft_ref):
     block = mask_ref.shape[1]
-    blocks = block // SUB
     u_ref[...] = w_ref[:, :block].astype(jnp.float32).T
     factor = f_ref[:, :block]
     eye = lax.broadcasted_iota(jnp.int32, (block, block), 0) == lax.broadcasted_iota(
@@ -25,8 +23,13 @@
     diagonal = jnp.sum(jnp.where(eye, factor, 0.0), axis=1, keepdims=True)
     m_ref[...] = (1 - mask_ref[...]).astype(jnp.float32).T * (1.0 / diagonal)
     factor_t = factor.T
-    for b in range(blocks):
+    for b in range(block // SUB):
         ft_ref[b, :, :SUB] = factor_t[:, b * SUB : (b + 1) * SUB]
+
+
+def prune_columns(first, last, u_ref, e_ref, m_ref, ft_ref):
+    block, rows = u_ref.shape
+    blocks = block // SUB
 
     def outer(b, carry):
         start = pl.multiple_of(b * SUB, SUB)
@@ -56,7 +59,12 @@
 
         return lax.fori_loop(b + 1, blocks, inner, carry)
 
-    lax.fori_loop(0, blocks, outer, 0)
+    lax.fori_loop(first, last, outer, 0)
+
+
+def prune_trailing(w_ref, f_ref, out_ref, u_ref, e_ref, lhs_ref, rhs_ref):
+    width = w_ref.shape[1]
+    block = u_ref.shape[0]
     errors = e_ref[...].T
     high = errors.astype(jnp.bfloat16)
     low = (errors - high.astype(jnp.float32)).astype(jnp.bfloat16)
@@ -80,6 +88,23 @@
     lax.fori_loop(0, (width - block) // tile, trail, 0)
 
 
+def prune_kernel(w_ref, mask_ref, f_ref, out_ref, u_ref, e_ref, m_ref, ft_ref, lhs_ref, rhs_ref):
+    prune_setup(w_ref, mask_ref, f_ref, u_ref, m_ref, ft_ref)
+    prune_columns(0, u_ref.shape[0] // SUB, u_ref, e_ref, m_ref, ft_ref)
+    prune_trailing(w_ref, f_ref, out_ref, u_ref, e_ref, lhs_ref, rhs_ref)
+
+
+def prune_scratch(rows, width, block):
+    return [
+        VMEM((block, rows), jnp.float32),
+        VMEM((block, rows), jnp.float32),
+        VMEM((block, rows), jnp.float32),
+        VMEM((block // SUB, block, LANES), jnp.float32),
+        VMEM((rows, 3 * block), jnp.bfloat16),
+        VMEM((3 * block, width), jnp.bfloat16),
+    ]
+
+
 def prune(weights, keep_mask, inv_factor):
     rows, width = weights.shape
     block = keep_mask.shape[1]
@@ -88,14 +113,7 @@
         out_shape=jax.ShapeDtypeStruct((rows, width), jnp.bfloat16),
         in_specs=[pl.BlockSpec(memory_space=VMEM)] * 3,
         out_specs=pl.BlockSpec(memory_space=VMEM),
-        scratch_shapes=[
-            VMEM((block, rows), jnp.float32),
-            VMEM((block, rows), jnp.float32),
-            VMEM((block, rows), jnp.float32),
-            VMEM((block // SUB, block, LANES), jnp.float32),
-            VMEM((rows, 3 * block), jnp.bfloat16),
-            VMEM((3 * block, width), jnp.bfloat16),
-        ],
+        scratch_shapes=prune_scratch(rows, width, block),
         cost_estimate=pl.CostEstimate(
             flops=6 * rows * block * width, bytes_accessed=4 * rows * width, transcendentals=0
         ),
@@ -103,36 +121,217 @@
     )(weights, keep_mask, inv_factor)
 
 
-def apply_kernel(capacity, token_rows, x_ref, w_ref, out_ref):
+def remote(src, dst, send_sem, recv_sem, device):
+    return pltpu.make_async_remote_copy(
+        src_ref=src,
+        dst_ref=dst,
+        send_sem=send_sem,
+        recv_sem=recv_sem,
+        device_id=device,
+        device_id_type=pl.DeviceIdType.MESH,
+    )
+
+
+def fused_kernel(
+    owners, capacity, own_ref, target_ref, w_any, mask_any, f_any, out_ref,
+    u_ref, e_ref, m_ref, ft_ref, lhs_ref, rhs_ref,
+    w_ref, mask_ref, f_ref, pruned_ref, tokens_ref, packed_ref, back_ref, pick_ref,
+    load_sem, line_sem, x_sem, y_sem, core_sem, in_sem, return_sem, back_sem,
+):
     width = w_ref.shape[1]
-    half = w_ref.shape[0] // 2
+    rows = own_ref.shape[0]
+    half_rows = rows // 2
+    devices = packed_ref.shape[0]
+    hidden_half = w_ref.shape[0] // 2
+    line = owners // 4
+    x = lax.axis_index("dp")
     expert = lax.axis_index("expert")
-    x = x_ref[:, :width]
-    both = lax.dot_general(
-        x, w_ref[...], (((1,), (1,)), ((), ())), preferred_element_type=jnp.float32
-    )
-    gate, up = both[:, :half], both[:, half:]
-    hidden = (gate / (1.0 + jnp.exp(-gate)) * up).astype(jnp.bfloat16)
-    ranks = x_ref[:, width:].astype(jnp.float32)
-    lane = lax.broadcasted_iota(jnp.int32, ranks.shape, 1)
-    rank = jnp.sum(jnp.where(lane == expert, ranks, 0.0), axis=1, keepdims=True).astype(jnp.int32)
-    slots = lax.broadcasted_iota(jnp.int32, (x.shape[0], capacity), 1)
-    pick = jnp.where(rank == slots, 1.0, 0.0).astype(jnp.bfloat16)
-    for j in range(x.shape[0] // token_rows):
-        part = slice(j * token_rows, (j + 1) * token_rows)
-        out_ref[j] = lax.dot_general(
-            pick[part], hidden[part], (((0,), (0,)), ((), ())), preferred_element_type=jnp.float32
+    z, y, core = expert // 4, (expert // 2) % 2, expert % 2
+    me = x * owners + expert
+    other_x, other_y, other_core = 1 - x, 1 - y, 1 - core
+
+    def expert_of(zz, yy, cc):
+        return zz * 4 + yy * 2 + cc
+
+    def part(n, first, count):
+        return tokens_ref.at[pl.ds(pl.multiple_of(n * rows + first, SUB * 2), count)]
+
+    x_to = (other_x, expert)
+    y_to = (x, expert_of(z, other_y, core))
+    core_to = (x, expert_of(z, y, other_core))
+
+    def level(r):
+        return (z + r) % line
+
+    def block_of(r, xx, yy, cc):
+        return xx * owners + expert_of(level(r), yy, cc)
+
+    def to_line(r):
+        there = (z + line - r) % line
+        return remote(
+            own_ref, part(me, 0, rows), line_sem.at[r], in_sem.at[me, 0],
+            (x, expert_of(there, y, core)),
+        )
+
+    def whole(src, n, sem, to):
+        return remote(src, part(n, 0, rows), sem, in_sem.at[n, 0], to)
+
+    def source(r):
+        return own_ref if isinstance(r, int) and r == 0 else part(block_of(r, x, y, core), 0, rows)
+
+    def plane_sends(r):
+        n = block_of(r, x, y, core)
+        return [
+            whole(source(r), n, x_sem.at[r, 0], x_to),
+            whole(source(r), n, y_sem.at[r, 0], y_to),
+            whole(source(r), n, core_sem.at[r, 0], core_to),
+        ]
+
+    def diagonal_sends(r):
+        n_y = block_of(r, x, other_y, core)
+        n_x = block_of(r, other_x, y, core)
+        upper, lower = part(n_y, 0, half_rows), part(n_x, half_rows, half_rows)
+        return [
+            remote(upper, upper, x_sem.at[r, 1], in_sem.at[n_y, 0], x_to),
+            remote(lower, lower, y_sem.at[r, 1], in_sem.at[n_x, 1], y_to),
+        ]
+
+    def side_sends(r):
+        n_y = block_of(r, x, other_y, core)
+        n_x = block_of(r, other_x, y, core)
+        return [
+            whole(part(n_y, 0, rows), n_y, core_sem.at[r, 1], core_to),
+            whole(part(n_x, 0, rows), n_x, core_sem.at[r, 2], core_to),
+        ]
+
+    def last_sends(r):
+        n = block_of(r, other_x, other_y, core)
+        return [whole(part(n, 0, rows), n, core_sem.at[r, 3], core_to)]
+
+    def arrive(n):
+        whole(part(n, 0, rows), n, core_sem.at[0, 0], core_to).wait_recv()
+
+    def arrive_half(n, h):
+        piece = part(n, h * half_rows, half_rows)
+        remote(piece, piece, core_sem.at[0, 0], in_sem.at[n, h], core_to).wait_recv()
+
+    def start(copies):
+        for copy in copies:
+            copy.start()
+
+    def first_stage(r):
+        arrive(block_of(r, x, y, core))
+        start(plane_sends(r))
+
+    def second_stage(r):
+        arrive(block_of(r, x, other_y, core))
+        arrive(block_of(r, other_x, y, core))
+        start(diagonal_sends(r) + side_sends(r))
+
+    def give_back(n):
+        return remote(
+            packed_ref.at[n], back_ref.at[me], return_sem.at[n], back_sem.at[me],
+            (n // owners, n % owners),
+        )
+
+    def apply(r):
+        n = block_of(r, other_x, other_y, core)
+        arrive_half(n, 0)
+        arrive_half(n, 1)
+        start(last_sends(r))
+        for xx in range(2):
+            for yy in range(2):
+                arrive(block_of(r, xx, yy, other_core))
+
+        def group(g, carry):
+            first = g * owners + level(r) * 4
+            span = pl.ds(pl.multiple_of(first * rows, SUB * 2), 4 * rows)
+            both = lax.dot_general(
+                tokens_ref[span, :width], pruned_ref[...], (((1,), (1,)), ((), ())),
+                preferred_element_type=jnp.float32,
+            )
+            gate, up = both[:, :hidden_half], both[:, hidden_half:]
+            hidden = (gate / (1.0 + jnp.exp(-gate)) * up).astype(jnp.bfloat16)
+            ranks = tokens_ref[span, width:].astype(jnp.float32)
+            lane = lax.broadcasted_iota(jnp.int32, ranks.shape, 1)
+            rank = jnp.sum(jnp.where(lane == expert, ranks, 0.0), axis=1, keepdims=True)
+            slots = lax.broadcasted_iota(jnp.int32, (4 * rows, capacity), 1).astype(jnp.float32)
+            pick = jnp.where(rank == slots, 1.0, 0.0).astype(jnp.bfloat16)
+            for j in range(4):
+                mine = slice(j * rows, (j + 1) * rows)
+                packed_ref[first + j] = lax.dot_general(
+                    pick[mine], hidden[mine], (((0,), (0,)), ((), ())),
+                    preferred_element_type=jnp.float32,
+                ).astype(jnp.bfloat16)
+            for j in range(4):
+                n = first + j
+
+                @pl.when(n == me)
+                def _():
+                    back_ref[me] = packed_ref[me]
+
+                @pl.when(n != me)
+                def _():
+                    give_back(n).start()
+
+            return carry
+
+        lax.fori_loop(0, 2, group, 0)
+
+    loads = [
+        pltpu.make_async_copy(w_any, w_ref, load_sem.at[0]),
+        pltpu.make_async_copy(mask_any, mask_ref, load_sem.at[1]),
+        pltpu.make_async_copy(f_any, f_ref, load_sem.at[2]),
+    ]
+    start(loads)
+    for r in range(1, line):
+        to_line(r).start()
+    start(plane_sends(0))
+    tokens_ref[pl.ds(pl.multiple_of(me * rows, SUB * 2), rows), :] = own_ref[...]
+    for load in loads:
+        load.wait()
+    blocks = u_ref.shape[0] // SUB
+    prune_setup(w_ref, mask_ref, f_ref, u_ref, m_ref, ft_ref)
+    prune_columns(0, blocks // 2, u_ref, e_ref, m_ref, ft_ref)
+    second_stage(0)
+    prune_columns(blocks // 2, blocks, u_ref, e_ref, m_ref, ft_ref)
+    first_stage(1)
+    prune_trailing(w_ref, f_ref, pruned_ref, u_ref, e_ref, lhs_ref, rhs_ref)
+    second_stage(1)
+    apply(0)
+
+    def middle(r, carry):
+        first_stage(r)
+        second_stage(r)
+        apply(r - 1)
+        return carry
+
+    lax.fori_loop(2, line, middle, 0)
+    apply(line - 1)
+    place = lax.broadcasted_iota(jnp.int32, pick_ref.shape, 1)
+    pick_ref[...] = jnp.where(target_ref[...] == place, 1.0, 0.0).astype(jnp.bfloat16)
+
+    def settle(n, carry):
+        @pl.when(n != me)
+        def _():
+            remote(
+                packed_ref.at[n], back_ref.at[n], return_sem.at[n], back_sem.at[n], x_to
+            ).wait_recv()
+            give_back(n).wait_send()
+
+        return carry
+
+    lax.fori_loop(0, devices, settle, 0)
+    for h in range(2):
+        got = back_ref[pl.ds(h * owners, owners)].reshape(owners * capacity, hidden_half)
+        out_ref[:, h * hidden_half : (h + 1) * hidden_half] = jnp.dot(
+            pick_ref[...], got, preferred_element_type=jnp.float32
         ).astype(jnp.bfloat16)
-
-
-def combine_kernel(target_ref, got_ref, out_ref):
-    halves, slots, half = got_ref.shape
-    place = lax.broadcasted_iota(jnp.int32, (target_ref.shape[0], slots), 1)
-    pick = jnp.where(target_ref[...] == place, 1.0, 0.0).astype(jnp.bfloat16)
-    for h in range(halves):
-        out_ref[:, h * half : (h + 1) * half] = jnp.dot(
-            pick, got_ref[h], preferred_element_type=jnp.float32
-        ).astype(jnp.bfloat16)
+    for r in range(line):
+        if r:
+            to_line(r).wait_send()
+        for copy in plane_sends(r) + diagonal_sends(r) + side_sends(r) + last_sends(r):
+            copy.wait_send()
 
 
 def ranks_of(routes, owners):
@@ -144,41 +343,55 @@
     return jnp.where(hot, rank, -1.0)
 
 
-def dense(tokens, routes, pruned, capacity):
+def dense(tokens, routes, weights, keep_mask, inv_factor, capacity):
     owners, groups = lax.axis_size("expert"), lax.axis_size("dp")
     token_rows, width = tokens.shape
     top = routes.shape[1]
     devices = owners * groups
-    half = pruned.shape[0] // 2
+    block = keep_mask.shape[1]
+    rows = weights.shape[0]
+    half = rows // 2
+    line = owners // 4
     rank = ranks_of(routes, owners)
     extra = -owners % LANES
     tagged = jnp.concatenate(
         [tokens, jnp.pad(rank, ((0, 0), (0, extra))).astype(jnp.bfloat16)], axis=1
     )
-    gathered = lax.all_gather(tagged, ("dp", "expert"), axis=0, tiled=True)
-    many = next(m for m in (4, 2, 1) if devices % m == 0)
-    packed = pl.pallas_call(
-        functools.partial(apply_kernel, capacity, token_rows),
-        grid=(devices // many,),
-        out_shape=jax.ShapeDtypeStruct((devices, capacity, half), jnp.bfloat16),
-        in_specs=[
-            pl.BlockSpec((many * token_rows, tagged.shape[1]), lambda i: (i, 0)),
-            pl.BlockSpec((2 * half, width), lambda i: (0, 0)),
-        ],
-        out_specs=pl.BlockSpec((many, capacity, half), lambda i: (i, 0, 0)),
-        name="apply",
-    )(gathered, pruned)
-    got = lax.all_to_all(packed, ("dp", "expert"), split_axis=0, concat_axis=0, tiled=True)
     ids = jnp.arange(owners, dtype=jnp.int32)
     own_rank = jnp.sum(
         jnp.where(routes[:, :, None] == ids[None, None, :], rank[:, None, :], 0.0), axis=2
     ).astype(jnp.int32)
     target = (routes * capacity + own_rank).reshape(-1, 1)
+    dma = pltpu.SemaphoreType.DMA
     out = pl.pallas_call(
-        combine_kernel,
+        functools.partial(fused_kernel, owners, capacity),
         out_shape=jax.ShapeDtypeStruct((token_rows * top, groups * half), jnp.bfloat16),
-        name="combine",
-    )(target, got.reshape(groups, owners * capacity, half))
+        in_specs=[pl.BlockSpec(memory_space=VMEM)] * 2 + [pl.BlockSpec(memory_space=pl.ANY)] * 3,
+        out_specs=pl.BlockSpec(memory_space=VMEM),
+        scratch_shapes=prune_scratch(rows, width, block)
+        + [
+            VMEM(weights.shape, weights.dtype),
+            VMEM(keep_mask.shape, keep_mask.dtype),
+            VMEM(inv_factor.shape, inv_factor.dtype),
+            VMEM(weights.shape, jnp.bfloat16),
+            VMEM((devices * token_rows, tagged.shape[1]), jnp.bfloat16),
+            VMEM((devices, capacity, half), jnp.bfloat16),
+            VMEM((devices, capacity, half), jnp.bfloat16),
+            VMEM((token_rows * top, owners * capacity), jnp.bfloat16),
+            dma((3,)),
+            dma((line,)),
+            dma((line, 2)),
+            dma((line, 2)),
+            dma((line, 4)),
+            dma((devices, 2)),
+            dma((devices,)),
+            dma((devices,)),
+        ],
+        compiler_params=pltpu.CompilerParams(
+            has_side_effects=True, vmem_limit_bytes=60 << 20
+        ),
+        name="fused",
+    )(tagged, target, weights, keep_mask, inv_factor)
     return out.reshape(token_rows, top, groups * half)
 
 
@@ -219,14 +432,13 @@
     owners, groups = lax.axis_size("expert"), lax.axis_size("dp")
     token_rows, width = tokens.shape
     capacity = token_rows * routes.shape[1] * 4 // (3 * owners)
-    pruned = prune(
-        weights.reshape(-1, width),
-        keep_mask.reshape(-1, keep_mask.shape[-1]),
-        inv_factor.reshape(-1, width),
-    )
-    if 2 * owners * groups * tokens.size <= GATHER_LIMIT:
-        return dense(tokens, routes, pruned, capacity)
-    return routed(tokens, routes, pruned, capacity)
+    weights = weights.reshape(-1, width)
+    keep_mask = keep_mask.reshape(-1, keep_mask.shape[-1])
+    inv_factor = inv_factor.reshape(-1, width)
+    fits = 2 * owners * groups * tokens.size <= GATHER_LIMIT
+    if fits and groups == 2 and owners % 4 == 0 and owners >= 8 and token_rows % 32 == 0:
+        return dense(tokens, routes, weights, keep_mask, inv_factor, capacity)
+    return routed(tokens, routes, prune(weights, keep_mask, inv_factor), capacity)
 
 
 def solution(mesh):

time: 183 us -> 122 us (0.67)
  the two profiles are of different devices: /device:TPU:0 before, /device:TPU:15 now
where the time goes in v2:
time: 122 us
  Pallas kernels  114 us (93%)
  other arithmetic  3.91 us (3%)
  local copies, waits for them, and re-layouts  3.55 us (3%)
    pallas_call x1, Pallas kernels, dense(): pl.pallas_call(functools.partial(fused_kernel, owners, capacity), out_sha...  114 us

profile of v2, /device:TPU:15, one launch (start us, length us, event | category | flops | bytes accessed | tf_op | source)
XLA Modules:
  0.0 121.9 jit_solution(8215926135045644687)
XLA Ops:
  0.0 0.7 fusion.2
  0.7 0.1 copy.13
  0.8 0.2 fusion.10
  1.0 0.1 copy.15
  1.1 0.7 select_reduce_fusion
  1.8 0.7 convert_add_fusion
  2.5 0.1 copy.16
  2.6 0.9 reshape.22.target_ref
  3.5 1.8 %fusion.1.own_ref = bf16[96,2176]{1,0:T(8,128)(2,1)} fusion(bf16[96,16]{1,0:T(8,128)(2,1)S(1)} %get-tuple-element.5, bf16[96,2048]{1,0:T(8,128)(2,1)} %param.5), kind=kLoop, calls=%fused_computation.3 | loop fusion | flops 1253376 | bytes 814080 | tf_op jit(solution)/shard_map/concatenate | solution.py:357
  5.3 114.2 %fused.1 = bf16[768,768]{1,0:T(8,128)(2,1)} custom-call(bf16[96,2176]{1,0:T(8,128)(2,1)} %fusion.1.own_ref, s32[768,1]{1,0:T(8,128)} %reshape.22.target_ref, bf16[768,2048]{1,0:T(8,128)(2,1)} %bitcast.6, s32[768,128]{1,0:T(8,128)} %bitcast.8, f32[128,2048]{1,0:T(8,128)} %bitcast.7), custom_call_target="tpu_custom_call" | custom-call | tf_op jit(solution)/shard_map/fused/pallas_call | solution.py:366
  119.5 2.4 %copy.21 = bf16[96,8,768]{2,1,0:T(8,128)(2,1)} copy(bf16[96,8,768]{2,1,0:T(8,128)(2,1)} %bitcast.5) | data formatting | bytes 2359296
  (1 shorter events, 0.0 us)

commit v3 on v2

--- a/solution.py
+++ b/solution.py
@@ -133,10 +133,10 @@
 
 
 def fused_kernel(
-    owners, capacity, own_ref, target_ref, w_any, mask_any, f_any, out_ref,
+    owners, capacity, own_ref, own_rank_ref, target_ref, w_any, mask_any, f_any, out_ref,
     u_ref, e_ref, m_ref, ft_ref, lhs_ref, rhs_ref,
-    w_ref, mask_ref, f_ref, pruned_ref, tokens_ref, packed_ref, back_ref, pick_ref,
-    load_sem, line_sem, x_sem, y_sem, core_sem, in_sem, return_sem, back_sem,
+    w_ref, mask_ref, f_ref, pruned_ref, tokens_ref, ranks_ref, packed_ref, back_ref,
+    pick_ref, rank_sem, rank_in_sem, load_sem, line_sem, x_sem, y_sem, core_sem, in_sem, return_sem, back_sem,
 ):
     width = w_ref.shape[1]
     rows = own_ref.shape[0]
@@ -179,11 +179,19 @@
     def source(r):
         return own_ref if isinstance(r, int) and r == 0 else part(block_of(r, x, y, core), 0, rows)
 
+    def half_send(src, n, h, sem, to):
+        piece = part(n, h * half_rows, half_rows)
+        if src is own_ref:
+            return remote(src.at[pl.ds(h * half_rows, half_rows)], piece, sem, in_sem.at[n, h], to)
+        return remote(piece, piece, sem, in_sem.at[n, h], to)
+
     def plane_sends(r):
         n = block_of(r, x, y, core)
         return [
-            whole(source(r), n, x_sem.at[r, 0], x_to),
-            whole(source(r), n, y_sem.at[r, 0], y_to),
+            half_send(source(r), n, 1, x_sem.at[r, 0], x_to),
+            half_send(source(r), n, 0, y_sem.at[r, 0], y_to),
+            half_send(source(r), n, 0, x_sem.at[r, 2], x_to),
+            half_send(source(r), n, 1, y_sem.at[r, 2], y_to),
             whole(source(r), n, core_sem.at[r, 0], core_to),
         ]
 
@@ -224,9 +232,22 @@
         start(plane_sends(r))
 
     def second_stage(r):
-        arrive(block_of(r, x, other_y, core))
-        arrive(block_of(r, other_x, y, core))
-        start(diagonal_sends(r) + side_sends(r))
+        upward, across = diagonal_sends(r)
+        arrive_half(block_of(r, x, other_y, core), 0)
+        upward.start()
+        arrive_half(block_of(r, other_x, y, core), 1)
+        across.start()
+
+    def third_stage(r):
+        arrive_half(block_of(r, x, other_y, core), 1)
+        arrive_half(block_of(r, other_x, y, core), 0)
+        start(side_sends(r))
+
+    def rank_send(n):
+        return remote(
+            own_rank_ref.at[n % owners], ranks_ref.at[me], rank_sem.at[n], rank_in_sem.at[me],
+            (n // owners, n % owners),
+        )
 
     def give_back(n):
         return remote(
@@ -247,21 +268,17 @@
             first = g * owners + level(r) * 4
             span = pl.ds(pl.multiple_of(first * rows, SUB * 2), 4 * rows)
             both = lax.dot_general(
-                tokens_ref[span, :width], pruned_ref[...], (((1,), (1,)), ((), ())),
+                tokens_ref[span, :], pruned_ref[...], (((1,), (1,)), ((), ())),
                 preferred_element_type=jnp.float32,
             )
             gate, up = both[:, :hidden_half], both[:, hidden_half:]
             hidden = (gate / (1.0 + jnp.exp(-gate)) * up).astype(jnp.bfloat16)
-            ranks = tokens_ref[span, width:].astype(jnp.float32)
-            lane = lax.broadcasted_iota(jnp.int32, ranks.shape, 1)
-            rank = jnp.sum(jnp.where(lane == expert, ranks, 0.0), axis=1, keepdims=True)
-            slots = lax.broadcasted_iota(jnp.int32, (4 * rows, capacity), 1).astype(jnp.float32)
-            pick = jnp.where(rank == slots, 1.0, 0.0).astype(jnp.bfloat16)
+            slots = lax.broadcasted_iota(jnp.int32, (capacity, rows), 0).astype(jnp.float32)
             for j in range(4):
-                mine = slice(j * rows, (j + 1) * rows)
-                packed_ref[first + j] = lax.dot_general(
-                    pick[mine], hidden[mine], (((0,), (0,)), ((), ())),
-                    preferred_element_type=jnp.float32,
+                rank = ranks_ref[first + j][:, :rows]
+                pick = jnp.where(rank == slots, 1.0, 0.0).astype(jnp.bfloat16)
+                packed_ref[first + j] = jnp.dot(
+                    pick, hidden[j * rows : (j + 1) * rows], preferred_element_type=jnp.float32
                 ).astype(jnp.bfloat16)
             for j in range(4):
                 n = first + j
@@ -287,6 +304,13 @@
     for r in range(1, line):
         to_line(r).start()
     start(plane_sends(0))
+
+    def share_rank(k, carry):
+        rank_send((me + k) % devices).start()
+        return carry
+
+    lax.fori_loop(1, devices, share_rank, 0)
+    ranks_ref[me] = own_rank_ref[expert]
     tokens_ref[pl.ds(pl.multiple_of(me * rows, SUB * 2), rows), :] = own_ref[...]
     for load in loads:
         load.wait()
@@ -295,15 +319,30 @@
     prune_columns(0, blocks // 2, u_ref, e_ref, m_ref, ft_ref)
     second_stage(0)
     prune_columns(blocks // 2, blocks, u_ref, e_ref, m_ref, ft_ref)
+    third_stage(0)
     first_stage(1)
     prune_trailing(w_ref, f_ref, pruned_ref, u_ref, e_ref, lhs_ref, rhs_ref)
     second_stage(1)
+
+    def know_rank(n, carry):
+        @pl.when(n != me)
+        def _():
+            remote(
+                own_rank_ref.at[0], ranks_ref.at[n], rank_sem.at[n], rank_in_sem.at[n], x_to
+            ).wait_recv()
+            rank_send(n).wait_send()
+
+        return carry
+
+    lax.fori_loop(0, devices, know_rank, 0)
     apply(0)
+    third_stage(1)
 
     def middle(r, carry):
         first_stage(r)
         second_stage(r)
         apply(r - 1)
+        third_stage(r)
         return carry
 
     lax.fori_loop(2, line, middle, 0)
@@ -353,10 +392,7 @@
     half = rows // 2
     line = owners // 4
     rank = ranks_of(routes, owners)
-    extra = -owners % LANES
-    tagged = jnp.concatenate(
-        [tokens, jnp.pad(rank, ((0, 0), (0, extra))).astype(jnp.bfloat16)], axis=1
-    )
+    rank_rows = jnp.pad(rank.T, ((0, 0), (0, -token_rows % LANES)))[:, None, :]
     ids = jnp.arange(owners, dtype=jnp.int32)
     own_rank = jnp.sum(
         jnp.where(routes[:, :, None] == ids[None, None, :], rank[:, None, :], 0.0), axis=2
@@ -366,7 +402,7 @@
     out = pl.pallas_call(
         functools.partial(fused_kernel, owners, capacity),
         out_shape=jax.ShapeDtypeStruct((token_rows * top, groups * half), jnp.bfloat16),
-        in_specs=[pl.BlockSpec(memory_space=VMEM)] * 2 + [pl.BlockSpec(memory_space=pl.ANY)] * 3,
+        in_specs=[pl.BlockSpec(memory_space=VMEM)] * 3 + [pl.BlockSpec(memory_space=pl.ANY)] * 3,
         out_specs=pl.BlockSpec(memory_space=VMEM),
         scratch_shapes=prune_scratch(rows, width, block)
         + [
@@ -374,14 +410,17 @@
             VMEM(keep_mask.shape, keep_mask.dtype),
             VMEM(inv_factor.shape, inv_factor.dtype),
             VMEM(weights.shape, jnp.bfloat16),
-            VMEM((devices * token_rows, tagged.shape[1]), jnp.bfloat16),
+            VMEM((devices * token_rows, width), jnp.bfloat16),
+            VMEM((devices,) + rank_rows.shape[1:], jnp.float32),
             VMEM((devices, capacity, half), jnp.bfloat16),
             VMEM((devices, capacity, half), jnp.bfloat16),
             VMEM((token_rows * top, owners * capacity), jnp.bfloat16),
+            dma((devices,)),
+            dma((devices,)),
             dma((3,)),
             dma((line,)),
-            dma((line, 2)),
-            dma((line, 2)),
+            dma((line, 3)),
+            dma((line, 3)),
             dma((line, 4)),
             dma((devices, 2)),
             dma((devices,)),
@@ -391,7 +430,7 @@
             has_side_effects=True, vmem_limit_bytes=60 << 20
         ),
         name="fused",
-    )(tagged, target, weights, keep_mask, inv_factor)
+    )(tokens, rank_rows, target, weights, keep_mask, inv_factor)
     return out.reshape(token_rows, top, groups * half)
 
 

time: 122 us -> 120 us (0.984)
  other arithmetic: 3.91 us -> 2.13 us
    concatenate x1 -> x0, other arithmetic: 1.78 us -> none  [dense(): jnp.concatenate([tokens, jnp.pad(rank, ((0, 0), (0, extra))).astype(jnp.b...]
    pallas_call x1, Pallas kernels: 114 us -> 113 us  [dense(): pl.pallas_call(functools.partial(fused_kernel, owners, capacity), out_sha...]
where the time goes in v3:
time: 120 us; the launch traced here: 119 us
  Pallas kernels  113 us (94%)
  local copies, waits for them, and re-layouts  3.95 us (3%)
  other arithmetic  2.13 us (2%)
    pallas_call x1, Pallas kernels, dense(): pl.pallas_call(functools.partial(fused_kernel, owners, capacity), out_sha...  113 us

profile of v3, /device:TPU:15, one launch (start us, length us, event | category | flops | bytes accessed | tf_op | source)
XLA Modules:
  0.0 119.2 jit_solution(8522745918236142780)
XLA Ops:
  0.0 0.7 fusion
  0.7 0.2 convolution_select_fusion
  0.9 0.7 select_reduce_fusion
  1.6 0.7 convert_add_fusion
  2.3 0.6 pad.4
  2.9 0.1 copy.13
  3.0 0.9 reshape.22.target_ref
  3.9 112.9 %fused.1 = bf16[768,768]{1,0:T(8,128)(2,1)} custom-call(bf16[96,2048]{1,0:T(8,128)(2,1)} %own_ref.1, f32[16,1,128]{2,1,0:T(1,128)} %bitcast.11, s32[768,1]{1,0:T(8,128)} %reshape.22.target_ref, bf16[768,2048]{1,0:T(8,128)(2,1)} %bitcast.8, s32[768,128]{1,0:T(8,128)} %bitcast.10, f32[128,2048]{1,0:T(8,128)} %bitcast.9), custom_call_target="tpu_custom_call" | custom-call | tf_op jit(solution)/shard_map/fused/pallas_call | solution.py:402
  116.8 2.4 %copy.16 = bf16[96,8,768]{2,1,0:T(8,128)(2,1)} copy(bf16[96,8,768]{2,1,0:T(8,128)(2,1)} %bitcast.7) | data formatting | bytes 2359296
  (1 shorter events, 0.0 us)
